TPU v7x, 128 devices: a whole 4x4x4 slice. The times are simulated.
128 devices in a mesh: seq: 16 (over z, x), tp: 8 (over y, core).
Axes of the slice: x: 4, y: 4, z: 4, core: 2. Of those that a mesh axis runs over, the one named last changes fastest.
Arguments:
- tokens: bfloat16 [2048, 6144], P('seq', 'tp'), may hold values from -6 to 6
- router_weight: bfloat16 [6144, 8], P('tp'), may hold values from -0.15625 to 0.15625
- expert_ids: int32 [2048, 2], P('seq'), may hold values from 0 to 7, all different within a row; in each aligned block of 128 rows (0 to 127, 128 to 255, ...) at most 56 rows name the same one
- gate_weight: bfloat16 [16, 6144, 4096], P('seq', None, 'tp'), may hold values from -0.078125 to 0.078125
- up_weight: bfloat16 [16, 6144, 4096], P('seq', None, 'tp'), may hold values from -0.078125 to 0.078125
- down_weight: bfloat16 [16, 4096, 6144], P('seq', 'tp'), may hold values from -0.0625 to 0.0625
Outputs:
- mixed: bfloat16 [2048, 6144], P('seq', 'tp')
Inputs may be any that keep to these rules, and one draw needn't show every extreme that they name: `expert_ids`: each row names 2 different experts. In each aligned block of 128 rows (the tokens of one sequence group) no expert is named more than 56 times, a bound that some block reaches.
All inputs are finite; a program needn't handle non-finite values.
Results may differ from a plain program's by a relative error of at most 0.014.
Values may be sent and summed in bfloat16 or wider, within the bound.
No kernel may reach another device: no remote copies, remote signals or barrier semaphores. Data moves between devices by JAX's collectives and lax.ppermute only.
A program may use at most 128 MiB of HBM per device.

v0:
```python
import jax
import jax.numpy as jnp
from jax import lax
from jax.sharding import PartitionSpec as P

D = 6144
CAP = 56


def sent_to_all(array, axis):
    length = lax.axis_size(axis)
    return lax.all_to_all(
        jnp.broadcast_to(array[None], (length, *array.shape)), axis, 0, 0, tiled=True
    )


def over_copies(array, axis):
    return sent_to_all(array, axis).sum(axis=0)


def slot_numbers(expert_ids, experts):
    flat_ids = expert_ids.reshape(-1)
    onehot = (flat_ids[:, None] == jnp.arange(experts, dtype=jnp.int32)[None, :]).astype(jnp.int32)
    before = jnp.cumsum(onehot, axis=0) - onehot
    return (flat_ids, jnp.sum(before * onehot, axis=1))


def per_device(tokens, router_weight, expert_ids, gate_weight, up_weight, down_weight):
    seq_count = lax.axis_size("seq")
    experts = router_weight.shape[1]
    halves = seq_count // experts
    tok_rows, top_count = expert_ids.shape
    capacity = CAP
    width = D
    gate_slab = gate_weight[0]
    up_slab = up_weight[0]
    down_slab = down_weight[0]
    partial_logits = jnp.dot(tokens, router_weight, preferred_element_type=jnp.float32)
    logits = over_copies(partial_logits, "tp")
    chosen = expert_ids[:, :, None] == jnp.arange(experts, dtype=jnp.int32)[None, None, :]
    picked = jnp.sum(jnp.where(chosen, logits[:, None, :], 0.0), axis=2)
    gates = jax.nn.sigmoid(picked - picked[:, ::-1])
    flat_ids, slots = slot_numbers(expert_ids, experts)
    row_index = jnp.arange(seq_count * capacity, dtype=jnp.int32)
    row_expert = row_index // capacity // halves
    row_slot = row_index % capacity
    matches = (row_expert[:, None] == flat_ids[None, :]) & (row_slot[:, None] == slots[None, :])
    select = jnp.any(matches.reshape(seq_count * capacity, tok_rows, top_count), axis=2).astype(
        jnp.bfloat16
    )
    outgoing = jnp.dot(select, tokens, preferred_element_type=jnp.float32).astype(jnp.bfloat16)
    outgoing = outgoing.reshape(seq_count, capacity, tokens.shape[1])
    received = lax.all_to_all(outgoing, "seq", split_axis=0, concat_axis=0, tiled=True)
    count = received.shape[1]
    piece = lax.all_gather(received, "tp", axis=2, tiled=True)
    piece_rows = piece.reshape(-1, piece.shape[2])
    gate = jnp.dot(piece_rows, gate_slab, preferred_element_type=jnp.float32)
    up = jnp.dot(piece_rows, up_slab, preferred_element_type=jnp.float32)
    hidden = (jax.nn.silu(gate) * up).astype(jnp.bfloat16)
    partial_value = jnp.dot(hidden, down_slab, preferred_element_type=jnp.float32).reshape(
        seq_count, count, width
    )
    reduced = lax.psum_scatter(
        partial_value.astype(jnp.bfloat16), "tp", scatter_dimension=2, tiled=True
    ).astype(jnp.float32)
    returned = lax.all_to_all(
        reduced.astype(jnp.bfloat16), "seq", split_axis=0, concat_axis=0, tiled=True
    ).astype(reduced.dtype)
    columns = returned.shape[2]
    summed = jnp.sum(returned.reshape(experts, halves, capacity, columns), axis=1)
    summed = summed.reshape(experts * capacity, columns)
    gathered = summed[flat_ids * capacity + slots].reshape(tok_rows, top_count, columns)
    mixed = jnp.sum(gathered * gates[:, :, None], axis=1)
    return mixed.astype(jnp.bfloat16)


def solution(mesh):
    in_specs = (
        P("seq", "tp"),
        P("tp", None),
        P("seq", None),
        P("seq", None, "tp"),
        P("seq", None, "tp"),
        P("seq", "tp", None),
    )
    out_specs = P("seq", "tp")
    return jax.shard_map(
        per_device, mesh=mesh, in_specs=in_specs, out_specs=out_specs, check_vma=False
    )
```

profile of v0, /device:TPU:9, one launch (start us, length us, event | category | flops | bytes accessed | tf_op | source)
XLA Modules:
  0.0 233.1 jit_solution(17153037409730043633)
XLA Ops:
  6.5 0.0 copy-start
  6.5 0.8 copy.27
  7.4 0.1 eq.78
  7.5 0.1 eq.74
  7.7 0.6 reduce-window.6
  8.3 0.2 slice_reduce_fusion
  8.5 0.1 fusion.8
  8.6 0.1 eq.82
  8.8 0.1 copy.29
  8.8 1.0 and_reduce_fusion
  9.9 0.5 convolution_convert_fusion.1
  10.4 27.4 %all_to_all.15 = bf16[16,56,768]{2,1,0:T(8,128)(2,1)} all-to-all(bf16[16,56,768]{2,1,0:T(8,128)(2,1)S(1)} %bitcast.37), channel_id=1, replica_groups=mesh['seq'=16,'tp'=8] {'seq'}, dimensions={0} | all-to-all | bytes 2752512 | tf_op jit(solution)/shard_map/all_to_all | solution.py:53
  37.8 0.0 all-gather.2.cloned.1.call-update
  37.8 0.0 reduce-scatter.2.cloned.1.call-start
  37.8 59.0 %all-gather.2.cloned.1.call-done = bf16[16,56,6144]{2,1,0:T(8,128)(2,1)} async-done(((bf16[16,56,768]{2,1,0:T(8,128)(2,1)}), bf16[16,56,6144]{2,1,0:T(8,128)(2,1)}) %all-gather.2.cloned.1.call-update) | async-done | bytes 11010064 | tf_op jit(solution)/shard_map/all_gather | solution.py:55
  96.9 10.6 %fusion.3 = f32[896,512]{1,0:T(8,128)S(1)} fusion(bf16[896,6144]{1,0:T(8,128)(2,1)} %bitcast.40, bf16[1,6144,512]{2,1,0:T(8,128)(2,1)} %param.9), kind=kOutput, calls=%fused_computation.5 | convolution fusion | flops 5637144576 | bytes 19136512 | tf_op jit(solution)/shard_map/dot_general | solution.py:57
  107.5 8.0 %multiply_convert_fusion = bf16[896,512]{1,0:T(8,128)(2,1)S(1)} fusion(f32[896,512]{1,0:T(8,128)S(1)} %fusion.3, bf16[896,6144]{1,0:T(8,128)(2,1)S(1)} %bitcast.41, bf16[1,6144,512]{2,1,0:T(8,128)(2,1)} %param.10), kind=kOutput, calls=%fused_computation.8 | convolution fusion | flops 5639897088 | bytes 20054016 | tf_op jit(solution)/shard_map/dot_general | solution.py:58
  115.5 11.3 %convolution_convert_fusion = bf16[16,56,6144]{2,1,0:T(8,128)(2,1)} fusion(bf16[16,56,512]{2,1,0:T(8,128)(2,1)S(1)} %bitcast.42, bf16[1,512,6144]{2,1,0:T(8,128)(2,1)} %param.11), kind=kOutput, calls=%fused_computation.1 | convolution fusion | flops 5642649600 | bytes 18219008 | tf_op jit(solution)/shard_map/dot_general | solution.py:60
  126.8 0.0 reduce-scatter.2.cloned.1.call-update
  126.9 0.7 copy-done.2
  127.5 0.1 fusion.19
  127.7 7.9 %all_to_all.16 = f32[8,128,8]{1,2,0:T(8,128)S(1)} all-to-all(f32[8,128,8]{1,2,0:T(8,128)S(1)} %broadcast_in_dim.10), channel_id=1, replica_groups=mesh['seq'=16,'tp'=8] {'tp'}, dimensions={0} | all-to-all | bytes 65536 | tf_op jit(solution)/shard_map/all_to_all | solution.py:12
  135.6 56.1 %reduce-scatter.2.cloned.1.call-done = bf16[16,56,768]{2,1,0:T(8,128)(2,1)} async-done(((bf16[16,56,6144]{2,1,0:T(8,128)(2,1)}), bf16[16,56,768]{2,1,0:T(8,128)(2,1)}) %reduce-scatter.2.cloned.1.call-update) | async-done | bytes 1376272 | tf_op jit(solution)/shard_map/reduce_scatter | solution.py:63
  191.7 6.7 %all-to-all-start.1 = ((bf16[16,56,768]{2,1,0:T(8,128)(2,1)}), bf16[16,56,768]{2,1,0:T(8,128)(2,1)S(1)}, u32[]{:S(2)}, u32[]{:S(2)}) async-start(bf16[16,56,768]{2,1,0:T(8,128)(2,1)} %reduce-scatter.2.cloned.1.call-done), calls=%async_computation.2 | async-start | bytes 2752512 | tf_op jit(solution)/shard_map/all_to_all | solution.py:66
  198.4 0.1 copy.30
  198.5 0.1 mul.39
  198.7 0.1 copy.31
  198.8 24.0 %all-to-all-done.1 = bf16[16,56,768]{2,1,0:T(8,128)(2,1)S(1)} async-done(((bf16[16,56,768]{2,1,0:T(8,128)(2,1)}), bf16[16,56,768]{2,1,0:T(8,128)(2,1)S(1)}, u32[]{:S(2)}, u32[]{:S(2)}) %all-to-all-start.1) | async-done | bytes 1376288 | tf_op jit(solution)/shard_map/all_to_all | solution.py:66
  222.8 0.2 convert_reduce_fusion
  223.0 1.1 gather_fusion
  224.1 0.5 reshape.133
  224.6 1.7 multiply_reduce_fusion
  (19 shorter events, 0.2 us)
Async XLA Ops:
  6.5 3.3 %copy-start = (bf16[128,768]{1,0:T(8,128)(2,1)S(1)}, bf16[128,768]{1,0:T(8,128)(2,1)}, u32[]{:S(2)}) copy-start(bf16[128,768]{1,0:T(8,128)(2,1)} %param.6) | copy-start | bytes 589828
  6.5 90.3 %all-gather.2.cloned.1.call-start = ((), (), s32[]{:S(2)}) async-start(), calls=%async_computation.4 | async-start | bytes 12386304 | tf_op jit(solution)/shard_map/all_gather | solution.py:55
  37.8 153.9 %reduce-scatter.2.cloned.1.call-start = ((), (), s32[]{:S(2)}) async-start(), calls=%async_computation.5 | async-start | bytes 12386304 | tf_op jit(solution)/shard_map/reduce_scatter | solution.py:63
  96.9 10.6 %copy-start.3 = (bf16[16,56,6144]{2,1,0:T(8,128)(2,1)S(1)}, bf16[16,56,6144]{2,1,0:T(8,128)(2,1)}, u32[]{:S(2)}) copy-start(bf16[16,56,6144]{2,1,0:T(8,128)(2,1)} %all-gather.2.cloned.1.call-done) | copy-start | bytes 33030148
  126.8 0.7 copy-start.2
  126.8 71.5 %copy-start.1 = (s32[128,2]{0,1:T(2,128)S(1)}, s32[128,2]{0,1:T(2,128)}, u32[]{:S(2)}) copy-start(s32[128,2]{0,1:T(2,128)} %param.8) | copy-start | bytes 3076
  191.7 31.1 %all-to-all-start.1 = ((bf16[16,56,768]{2,1,0:T(8,128)(2,1)}), bf16[16,56,768]{2,1,0:T(8,128)(2,1)S(1)}, u32[]{:S(2)}, u32[]{:S(2)}) async-start(bf16[16,56,768]{2,1,0:T(8,128)(2,1)} %reduce-scatter.2.cloned.1.call-done), calls=%async_computation.2 | async-start | bytes 2752512 | tf_op jit(solution)/shard_map/all_to_all | solution.py:66
Sparse Core Ops, SparseCore 0:
  37.9 58.9 all-gather.1
  127.0 64.6 reduce-scatter.1
where the time goes:
time: 233 us
  waiting for transfers between devices  139 us (60%)
  blocking collectives  35.3 us (15%)
  matrix products  30.6 us (13%)
  between operations  13.6 us (6%)
  starting transfers between devices  6.71 us (3%)
  local copies, waits for them, and re-layouts  4.17 us (2%)
  other arithmetic  3.74 us (2%)
    all_gather x1, waiting for transfers between devices, per_device(): piece = lax.all_gather(received, 'tp', axis=2, tiled=True)  59 us
    reduce_scatter x1, waiting for transfers between devices, per_device(): lax.psum_scatter(partial_value.astype(jnp.bfloat16), 'tp', scatter_dimens...  56.1 us
    all_to_all x1, blocking collectives, per_device(): lax.all_to_all(outgoing, 'seq', split_axis=0, concat_axis=0, tiled=True)  27.4 us
    all_to_all x1, waiting for transfers between devices, per_device(): lax.all_to_all(reduced.astype(jnp.bfloat16), 'seq', split_axis=0, concat_...  24 us
    dot_general x1, matrix products, per_device(): jnp.dot(hidden, down_slab, preferred_element_type=jnp.float32)  11.3 us
    dot_general x1, matrix products, per_device(): gate = jnp.dot(piece_rows, gate_slab, preferred_element_type=jnp.float32)  10.6 us
    dot_general x1, matrix products, per_device(): up = jnp.dot(piece_rows, up_slab, preferred_element_type=jnp.float32)  8.03 us
    all_to_all x1, blocking collectives, sent_to_all(): lax.all_to_all(jnp.broadcast_to(array[None], (length, *array.shape)), axi...  7.9 us
  transfers between devices with their start and end apart: 3, of which 3 were waited for; matrix products, arithmetic and copies ran while one was open for 0% of the time, Pallas kernels for 0%

commit v1 on v0

--- a/solution.py
+++ b/solution.py
@@ -5,6 +5,10 @@
 
 D = 6144
 CAP = 56
+clear_stages_all = lambda dev_axis, dim_no, x_part: jnp.concatenate(
+    lax.all_to_all(jnp.stack([x_part for _ in range(lax.axis_size(dev_axis))]), dev_axis, 0, 0),
+    dim_no,
+)
 
 
 def sent_to_all(array, axis):
@@ -52,7 +56,7 @@
     outgoing = outgoing.reshape(seq_count, capacity, tokens.shape[1])
     received = lax.all_to_all(outgoing, "seq", split_axis=0, concat_axis=0, tiled=True)
     count = received.shape[1]
-    piece = lax.all_gather(received, "tp", axis=2, tiled=True)
+    piece = clear_stages_all("tp", 2, received)
     piece_rows = piece.reshape(-1, piece.shape[2])
     gate = jnp.dot(piece_rows, gate_slab, preferred_element_type=jnp.float32)
     up = jnp.dot(piece_rows, up_slab, preferred_element_type=jnp.float32)

time: 233 us -> 324 us (1.39)
  blocking collectives: 35.3 us -> 163 us
  waiting for transfers between devices: 139 us -> 76.3 us
  local copies, waits for them, and re-layouts: 4.17 us -> 34.7 us
  matrix products: 30.6 us -> 25.8 us
    all_to_all x0 -> x1, blocking collectives: none -> 128 us  [lax.all_to_all(jnp.stack([x_part for _ in range(lax.axis_size(dev_axis))]...]
    all_gather x1 -> x0, waiting for transfers between devices: 59 us -> none  [per_device(): piece = lax.all_gather(received, 'tp', axis=2, tiled=True)]
    reshape x0 -> x1, local copies, waits for them, and re-layouts: none -> 22.3 us  [jnp.concatenate(lax.all_to_all(jnp.stack([x_part for _ in range(lax.axis_...]
    another operation x1 -> x2, local copies, waits for them, and re-layouts: 0.01 us -> 4.92 us  [the longest x1 4.92 us: jnp.stack([x_part for _ in range(lax.axis_size(dev_axis))])]
    dot_general x1, matrix products: 10.6 us -> 5.83 us  [per_device(): gate = jnp.dot(piece_rows, gate_slab, preferred_element_type=jnp.float32)]
    reduce_scatter x1, waiting for transfers between devices: 56.1 us -> 52.3 us  [per_device(): lax.psum_scatter(partial_value.astype(jnp.bfloat16), 'tp', scatter_dimens...]
    unnamed x9 -> x12, local copies, waits for them, and re-layouts: 1.52 us -> 4.77 us
  transfers between devices with their start and end apart: 3 -> 2, of which waited for: 3 -> 2; matrix products, arithmetic and copies ran while one was open for 0% -> 0% of each run, Pallas kernels for 0% -> 0%
where the time goes in v1:
time: 324 us
  blocking collectives  163 us (50%)
  waiting for transfers between devices  76.3 us (24%)
  local copies, waits for them, and re-layouts  34.7 us (11%)
  matrix products  25.8 us (8%)
  between operations  13.6 us (4%)
  starting transfers between devices  6.6 us (2%)
  other arithmetic  3.74 us (1%)
    all_to_all x1, blocking collectives, lax.all_to_all(jnp.stack([x_part for _ in range(lax.axis_size(dev_axis))]...  128 us
    reduce_scatter x1, waiting for transfers between devices, per_device(): lax.psum_scatter(partial_value.astype(jnp.bfloat16), 'tp', scatter_dimens...  52.3 us
    all_to_all x1, blocking collectives, per_device(): lax.all_to_all(outgoing, 'seq', split_axis=0, concat_axis=0, tiled=True)  27.2 us
    all_to_all x1, waiting for transfers between devices, per_device(): lax.all_to_all(reduced.astype(jnp.bfloat16), 'seq', split_axis=0, concat_...  24 us
    reshape x1, local copies, waits for them, and re-layouts, jnp.concatenate(lax.all_to_all(jnp.stack([x_part for _ in range(lax.axis_...  22.3 us
    dot_general x1, matrix products, per_device(): jnp.dot(hidden, down_slab, preferred_element_type=jnp.float32)  11.3 us
    dot_general x1, matrix products, per_device(): up = jnp.dot(piece_rows, up_slab, preferred_element_type=jnp.float32)  8.03 us
    all_to_all x1, blocking collectives, sent_to_all(): lax.all_to_all(jnp.broadcast_to(array[None], (length, *array.shape)), axi...  7.59 us
  transfers between devices with their start and end apart: 2, of which 2 were waited for; matrix products, arithmetic and copies ran while one was open for 0% of the time, Pallas kernels for 0%

profile of v1, /device:TPU:9, one launch (start us, length us, event | category | flops | bytes accessed | tf_op | source)
XLA Modules:
  0.0 324.0 jit_solution(17496300164440277337)
XLA Ops:
  6.5 0.8 copy.29
  7.4 0.1 eq.78
  7.5 0.1 eq.74
  7.7 0.6 reduce-window.6
  8.3 0.2 slice_reduce_fusion
  8.5 0.1 fusion.8
  8.6 0.1 eq.82
  8.8 0.1 copy.31
  8.8 1.0 and_reduce_fusion
  9.9 0.5 convolution_convert_fusion.1
  10.4 27.2 %all_to_all.20 = bf16[16,56,768]{2,1,0:T(8,128)(2,1)S(1)} all-to-all(bf16[16,56,768]{2,1,0:T(8,128)(2,1)S(1)} %bitcast.44), channel_id=1, replica_groups=mesh['seq'=16,'tp'=8] {'seq'}, dimensions={0} | all-to-all | bytes 2752512 | tf_op jit(solution)/shard_map/all_to_all | solution.py:57
  37.6 4.9 %stack.2 = bf16[8,16,56,768]{3,2,1,0:T(8,128)(2,1)} broadcast(bf16[16,56,768]{2,1,0:T(8,128)(2,1)S(1)} %all_to_all.20), dimensions={1,2,3} | broadcast | bytes 12386304 | tf_op jit(solution)/shard_map/stack | solution.py:9
  42.6 128.4 %all_to_all.21 = bf16[8,16,56,768]{3,2,1,0:T(8,128)(2,1)S(1)} all-to-all(bf16[8,16,56,768]{3,2,1,0:T(8,128)(2,1)} %stack.2), channel_id=1, replica_groups=mesh['seq'=16,'tp'=8] {'tp'}, dimensions={0} | all-to-all | bytes 22020096 | tf_op jit(solution)/shard_map/all_to_all | solution.py:9
  171.0 22.3 %copy.32 = bf16[16,56,8,768]{3,2,1,0:T(8,128)(2,1)S(1)} copy(bf16[16,56,8,768]{3,1,0,2:T(8,128)(2,1)S(1)} %bitcast.39) | data formatting | bytes 22020096 | tf_op jit(solution)/shard_map/reshape | solution.py:8
  193.3 3.2 %copy.35 = bf16[112,8,8,768]{3,1,2,0:T(8,128)(2,1)S(1)} copy(bf16[112,8,8,768]{3,2,1,0:T(8,128)(2,1)S(1)} %bitcast.40) | data formatting | bytes 22020096
  196.6 5.8 %fusion.3 = f32[896,512]{1,0:T(8,128)S(1)} fusion(bf16[896,6144]{1,0:T(8,128)(2,1)S(1)} %bitcast.42, bf16[1,6144,512]{2,1,0:T(8,128)(2,1)S(1)} %bitcast.48), kind=kOutput, calls=%fused_computation.5 | convolution fusion | flops 5637144576 | bytes 19136512 | tf_op jit(solution)/shard_map/dot_general | solution.py:61
  202.4 8.0 %multiply_convert_fusion = bf16[896,512]{1,0:T(8,128)(2,1)S(1)} fusion(f32[896,512]{1,0:T(8,128)S(1)} %fusion.3, bf16[896,6144]{1,0:T(8,128)(2,1)S(1)} %bitcast.43, bf16[1,6144,512]{2,1,0:T(8,128)(2,1)} %param.10), kind=kOutput, calls=%fused_computation.8 | convolution fusion | flops 5639897088 | bytes 20054016 | tf_op jit(solution)/shard_map/dot_general | solution.py:62
  210.5 11.3 %convolution_convert_fusion = bf16[16,56,6144]{2,1,0:T(8,128)(2,1)} fusion(bf16[16,56,512]{2,1,0:T(8,128)(2,1)S(1)} %bitcast.49, bf16[1,512,6144]{2,1,0:T(8,128)(2,1)} %param.11), kind=kOutput, calls=%fused_computation.1 | convolution fusion | flops 5642649600 | bytes 18219008 | tf_op jit(solution)/shard_map/dot_general | solution.py:64
  221.8 0.0 reduce-scatter.2.cloned.1.call-update
  221.8 0.7 copy-done.2
  222.5 0.1 fusion.19
  222.6 7.6 %all_to_all.22 = f32[8,128,8]{1,2,0:T(8,128)S(1)} all-to-all(f32[8,128,8]{1,2,0:T(8,128)S(1)} %broadcast_in_dim.10), channel_id=1, replica_groups=mesh['seq'=16,'tp'=8] {'tp'}, dimensions={0} | all-to-all | bytes 65536 | tf_op jit(solution)/shard_map/all_to_all | solution.py:16
  230.2 52.3 %reduce-scatter.2.cloned.1.call-done = bf16[16,56,768]{2,1,0:T(8,128)(2,1)} async-done(((bf16[16,56,6144]{2,1,0:T(8,128)(2,1)}), bf16[16,56,768]{2,1,0:T(8,128)(2,1)}) %reduce-scatter.2.cloned.1.call-update) | async-done | bytes 1376272 | tf_op jit(solution)/shard_map/reduce_scatter | solution.py:67
  282.6 6.6 %all-to-all-start.2 = ((bf16[16,56,768]{2,1,0:T(8,128)(2,1)}), bf16[16,56,768]{2,1,0:T(8,128)(2,1)S(1)}, u32[]{:S(2)}, u32[]{:S(2)}) async-start(bf16[16,56,768]{2,1,0:T(8,128)(2,1)} %reduce-scatter.2.cloned.1.call-done), calls=%async_computation.3 | async-start | bytes 2752512 | tf_op jit(solution)/shard_map/all_to_all | solution.py:70
  289.2 0.1 copy.33
  289.3 0.1 mul.39
  289.5 0.1 copy.34
  289.7 24.0 %all-to-all-done.2 = bf16[16,56,768]{2,1,0:T(8,128)(2,1)S(1)} async-done(((bf16[16,56,768]{2,1,0:T(8,128)(2,1)}), bf16[16,56,768]{2,1,0:T(8,128)(2,1)S(1)}, u32[]{:S(2)}, u32[]{:S(2)}) %all-to-all-start.2) | async-done | bytes 1376288 | tf_op jit(solution)/shard_map/all_to_all | solution.py:70
  313.6 0.2 convert_reduce_fusion
  313.9 1.1 gather_fusion
  315.0 0.5 reshape.135
  315.4 1.7 multiply_reduce_fusion
  (23 shorter events, 0.2 us)
Async XLA Ops:
  6.5 3.3 %copy-start = (bf16[128,768]{1,0:T(8,128)(2,1)S(1)}, bf16[128,768]{1,0:T(8,128)(2,1)}, u32[]{:S(2)}) copy-start(bf16[128,768]{1,0:T(8,128)(2,1)} %param.6) | copy-start | bytes 589828
  6.5 276.0 %reduce-scatter.2.cloned.1.call-start = ((), (), s32[]{:S(2)}) async-start(), calls=%async_computation.5 | async-start | bytes 12386304 | tf_op jit(solution)/shard_map/reduce_scatter | solution.py:67
  171.0 25.6 %slice-start = ((s8[6291456]{0:T(1024)(128)(4,1)}), s8[4194304]{0:T(1024)(128)(4,1)S(1)}, s32[]{:S(2)}) async-start(s8[6291456]{0:T(1024)(128)(4,1)} %bitcast.47), calls=%async_computation.6 | async-start | bytes 8388608
  193.3 3.3 %slice-start.1 = ((s8[6291456]{0:T(1024)(128)(4,1)}), s8[2097152]{0:T(1024)(128)(4,1)S(1)}, s32[]{:S(2)}) async-start(s8[6291456]{0:T(1024)(128)(4,1)} %bitcast.47), calls=%async_computation.7 | async-start | bytes 4194304
  221.8 0.7 copy-start.2
  221.8 67.4 %copy-start.1 = (s32[128,2]{0,1:T(2,128)S(1)}, s32[128,2]{0,1:T(2,128)}, u32[]{:S(2)}) copy-start(s32[128,2]{0,1:T(2,128)} %param.8) | copy-start | bytes 3076
  282.6 31.1 %all-to-all-start.2 = ((bf16[16,56,768]{2,1,0:T(8,128)(2,1)}), bf16[16,56,768]{2,1,0:T(8,128)(2,1)S(1)}, u32[]{:S(2)}, u32[]{:S(2)}) async-start(bf16[16,56,768]{2,1,0:T(8,128)(2,1)} %reduce-scatter.2.cloned.1.call-done), calls=%async_computation.3 | async-start | bytes 2752512 | tf_op jit(solution)/shard_map/all_to_all | solution.py:70
Sparse Core Ops, SparseCore 0:
  222.0 60.5 reduce-scatter.1
